TPU v7x, 32 devices: a whole 2x2x4 slice. The times are simulated.
32 devices in a mesh: seq: 4 (over y, core), fsdp: 8 (over z, x).
Axes of the slice: x: 2, y: 2, z: 4, core: 2. Of those that a mesh axis runs over, the one named last changes fastest.
Arguments:
- tokens: bfloat16 [8, 1024, 2048], P('fsdp', 'seq'), may hold values from -6 to 6
- teacher: bfloat16 [8, 1024, 2048], P('fsdp', 'seq'), may hold values from -6 to 6
- segments: int32 [8, 1024], P('fsdp'), may hold values from 0 to 3, never falling along the last dimension, each value on 1 to 512 neighbouring positions
- valid: int32 [8, 1024], P('fsdp', 'seq'), may hold values from 0 to 1, as said below
- ln1_gain: bfloat16 [2048], P('fsdp'), may hold values from 0.099609375 to 1.8984375
- ln1_bias: bfloat16 [2048], P('fsdp'), may hold values from -1.75 to 1.75
- w_qkv: bfloat16 [2048, 6144], P('fsdp'), may hold values from -0.125 to 0.125
- b_qkv: bfloat16 [6144], P('fsdp'), may hold values from -1.75 to 1.75
- w_out: bfloat16 [2048, 2048], P('fsdp'), may hold values from -0.5 to 0.5
- ln2_gain: bfloat16 [2048], P('fsdp'), may hold values from 0.099609375 to 1.8984375
- ln2_bias: bfloat16 [2048], P('fsdp'), may hold values from -1.75 to 1.75
- w_gate_up: bfloat16 [5632, 2, 2048], P('fsdp'), may hold values from -0.125 to 0.125
- w_down: bfloat16 [5632, 2048], P('fsdp'), may hold values from -0.15625 to 0.15625
Outputs:
- layer_out: bfloat16 [8, 1024, 2048], P('fsdp', 'seq')
- loss: float32 [], replicated
- grad_tokens: bfloat16 [8, 1024, 2048], P('fsdp', 'seq')
- grad_ln1_gain: float32 [2048], P('fsdp')
- grad_ln1_bias: float32 [2048], P('fsdp')
- grad_w_qkv: float32 [2048, 6144], P('fsdp')
- grad_b_qkv: float32 [6144], P('fsdp')
- grad_w_out: float32 [2048, 2048], P('fsdp')
- grad_ln2_gain: float32 [2048], P('fsdp')
- grad_ln2_bias: float32 [2048], P('fsdp')
- grad_w_gate_up: float32 [5632, 2, 2048], P('fsdp')
- grad_w_down: float32 [5632, 2048], P('fsdp')
Inputs may be any that keep to these rules, and one draw needn't show every extreme that they name: `segments`: segment numbers start at 0 in each sequence and never fall; each document has 1 to 512 tokens and one document of each sequence has exactly that many. `valid`: the first token of every sequence counts.
All inputs are finite; a program needn't handle non-finite values.
Results may differ from a plain program's by a relative error of at most 0.01.
Values may be sent and summed in bfloat16 or wider, within the bound.
No kernel may reach another device: no remote copies, remote signals or barrier semaphores. Data moves between devices by JAX's collectives and lax.ppermute only.
A program may use at most 704 MiB of HBM per device.

v0:
```python
import jax
import jax.numpy as jnp
from jax import lax
from jax.sharding import PartitionSpec as P

H = 32
HD = 64
ROT = 16
EPSILON = 1e-05
MASKED_VALUE = -1e30


def norm_parts(values):
    mean_value = jnp.mean(values, axis=-1, keepdims=True)
    centered = values - mean_value
    variance = jnp.mean(centered * centered, axis=-1, keepdims=True)
    inv_std = lax.rsqrt(variance + EPSILON)
    return (centered * inv_std, inv_std)


def norm_back(grad_out, normed, inv_std, gain_vec):
    scaled = grad_out * gain_vec
    mean_scaled = jnp.mean(scaled, axis=-1, keepdims=True)
    mean_cross = jnp.mean(scaled * normed, axis=-1, keepdims=True)
    return inv_std * (scaled - mean_scaled - normed * mean_cross)


def doc_positions(segment):
    places = jnp.arange(segment.shape[0], dtype=jnp.int32)
    change = jnp.concatenate([jnp.ones((1,), dtype=bool), segment[1:] != segment[:-1]])
    starts = lax.cummax(jnp.where(change, places, 0), axis=0)
    return places - starts


def rotate(values, positions, turn_sign):
    half_rot = ROT // 2
    inverse = 10000.0 ** (-(jnp.arange(half_rot, dtype=jnp.float32) * 2.0) / ROT)
    angles = positions.astype(jnp.float32)[:, None] * inverse[None, :]
    cosine = jnp.cos(angles)[:, None, :]
    sine_part = turn_sign * jnp.sin(angles)[:, None, :]
    front_half = values[..., :half_rot]
    back_half = values[..., half_rot:ROT]
    return jnp.concatenate(
        [
            front_half * cosine - back_half * sine_part,
            back_half * cosine + front_half * sine_part,
            values[..., ROT:],
        ],
        axis=-1,
    )


def gate_backward(gate_up, hidden_grad):
    gate_part = gate_up[:, 0]
    up_part = gate_up[:, 1]
    gate_sig = jax.nn.sigmoid(gate_part)
    up_grad = hidden_grad * (gate_part * gate_sig)
    silu_grad = hidden_grad * up_part
    gate_grad = silu_grad * gate_sig + silu_grad * gate_part * gate_sig * (1.0 - gate_sig)
    return jnp.stack([gate_grad, up_grad], axis=1).astype(jnp.bfloat16)


def block_scores(query_block, key_rows, block_seg, segment, first_row, score_scale):
    block_size = query_block.shape[0]
    places = jnp.arange(segment.shape[0], dtype=jnp.int32)
    block_places = first_row + jnp.arange(block_size, dtype=jnp.int32)
    allowed = (block_seg[:, None] == segment[None, :]) & (block_places[:, None] >= places[None, :])
    scores = (
        jnp.einsum("bhd,lhd->hbl", query_block, key_rows, preferred_element_type=jnp.float32)
        * score_scale
    )
    return jnp.where(allowed[None], scores, MASKED_VALUE)


def attention_forward(query_rows, key_rows, value_rows, segment, block_size, score_scale):
    length_total = key_rows.shape[0]

    def one_block(unused, first_row):
        query_block = lax.dynamic_slice_in_dim(query_rows, first_row, block_size, 0)
        block_seg = lax.dynamic_slice_in_dim(segment, first_row, block_size, 0)
        scores = block_scores(query_block, key_rows, block_seg, segment, first_row, score_scale)
        row_max = jnp.max(scores, axis=-1, keepdims=True)
        exp_scores = jnp.exp(scores - row_max)
        row_sum = jnp.sum(exp_scores, axis=-1, keepdims=True)
        probs = (exp_scores / row_sum).astype(jnp.bfloat16)
        block_out = jnp.einsum(
            "hbl,lhd->bhd", probs, value_rows, preferred_element_type=jnp.float32
        )
        return (unused, (block_out.astype(jnp.bfloat16), (row_max + jnp.log(row_sum))[..., 0]))

    firsts = jnp.arange(length_total // block_size, dtype=jnp.int32) * block_size
    unused, (block_outs, log_totals) = lax.scan(one_block, jnp.zeros((), jnp.int32), firsts)
    return (block_outs.reshape(length_total, query_rows.shape[1], query_rows.shape[2]), log_totals)


def attention_backward(
    query_rows, key_rows, value_rows, out_grad, log_totals, segment, block_size, score_scale
):
    length_total = key_rows.shape[0]

    def one_block(grad_carry, block_inputs):
        key_grad, value_grad = grad_carry
        first_row, block_log = block_inputs
        query_block = lax.dynamic_slice_in_dim(query_rows, first_row, block_size, 0)
        grad_block = lax.dynamic_slice_in_dim(out_grad, first_row, block_size, 0)
        block_seg = lax.dynamic_slice_in_dim(segment, first_row, block_size, 0)
        scores = block_scores(query_block, key_rows, block_seg, segment, first_row, score_scale)
        probs = jnp.exp(scores - block_log[..., None])
        prob_low = probs.astype(jnp.bfloat16)
        value_grad = value_grad + jnp.einsum(
            "hbl,bhd->lhd", prob_low, grad_block, preferred_element_type=jnp.float32
        )
        prob_grad = jnp.einsum(
            "bhd,lhd->hbl", grad_block, value_rows, preferred_element_type=jnp.float32
        )
        row_dot = jnp.sum(probs * prob_grad, axis=-1, keepdims=True)
        score_grad = (probs * (prob_grad - row_dot)).astype(jnp.bfloat16)
        query_grad = (
            jnp.einsum("hbl,lhd->bhd", score_grad, key_rows, preferred_element_type=jnp.float32)
            * score_scale
        )
        key_grad = (
            key_grad
            + jnp.einsum(
                "hbl,bhd->lhd", score_grad, query_block, preferred_element_type=jnp.float32
            )
            * score_scale
        )
        return ((key_grad, value_grad), query_grad)

    firsts = jnp.arange(length_total // block_size, dtype=jnp.int32) * block_size
    zero_grad = jnp.zeros(key_rows.shape, jnp.float32)
    (key_grad, value_grad), query_grads = lax.scan(
        one_block, (zero_grad, zero_grad), (firsts, log_totals)
    )
    return (query_grads.reshape(key_rows.shape), key_grad, value_grad)


def reduce_rows(term_rows, row_share):
    return lax.psum_scatter(
        term_rows(jnp.int32(0), row_share * lax.axis_size("fsdp")).astype(jnp.bfloat16),
        "fsdp",
        scatter_dimension=0,
        tiled=True,
    ).astype(jnp.float32)


def per_device(
    tokens,
    teacher,
    segments,
    valid,
    ln1_gain,
    ln1_bias,
    w_qkv,
    b_qkv,
    w_out,
    ln2_gain,
    ln2_bias,
    w_gate_up,
    w_down,
):
    seq_count = lax.axis_size("seq")
    fsdp_count = lax.axis_size("fsdp")
    seq_index = lax.axis_index("seq")
    fsdp_index = lax.axis_index("fsdp")
    row_count = tokens.shape[1]
    model_width = tokens.shape[2]
    length_total = segments.shape[1]
    heads_here = H // seq_count
    group_width = heads_here * HD
    block_size = min(512, length_total)
    score_scale = HD ** (-0.5)
    tokens_total = row_count * seq_count * fsdp_count
    full_qkv, full_out, full_bias, gain_one, shift_one, gain_two, shift_two = (
        lax.all_gather(w_qkv, "fsdp", axis=0, tiled=True),
        lax.all_gather(w_out, "fsdp", axis=0, tiled=True),
        lax.all_gather(b_qkv, "fsdp", axis=0, tiled=True),
        lax.all_gather(ln1_gain, "fsdp", axis=0, tiled=True),
        lax.all_gather(ln1_bias, "fsdp", axis=0, tiled=True),
        lax.all_gather(ln2_gain, "fsdp", axis=0, tiled=True),
        lax.all_gather(ln2_bias, "fsdp", axis=0, tiled=True),
    )
    gain_one = gain_one.astype(jnp.float32)
    gain_two = gain_two.astype(jnp.float32)
    segment = segments[0]
    positions_all = doc_positions(segment)
    positions = lax.dynamic_slice_in_dim(positions_all, seq_index * row_count, row_count, 0)
    tokens_in = tokens[0].astype(jnp.float32)
    teacher_in = teacher[0].astype(jnp.float32)
    counted = valid[0].astype(jnp.float32)
    normed_one, inv_std_one = norm_parts(tokens_in)
    hidden_one = (normed_one * gain_one + shift_one.astype(jnp.float32)).astype(jnp.bfloat16)
    qkv_float = jnp.dot(
        hidden_one, full_qkv, preferred_element_type=jnp.float32
    ) + full_bias.astype(jnp.float32)
    split_rows = qkv_float.reshape(row_count, 3, H, HD)
    packed = jnp.stack(
        [
            rotate(split_rows[:, 0], positions, 1.0),
            rotate(split_rows[:, 1], positions, 1.0),
            split_rows[:, 2],
        ],
        axis=1,
    )
    packed = packed.astype(jnp.bfloat16).reshape(row_count, 3, seq_count, group_width)
    spread = lax.all_to_all(packed, "seq", split_axis=2, concat_axis=0, tiled=True)
    head_rows = spread.reshape(length_total, 3, heads_here, HD)
    query_rows = head_rows[:, 0]
    key_rows = head_rows[:, 1]
    value_rows = head_rows[:, 2]
    heads_out, log_totals = attention_forward(
        query_rows, key_rows, value_rows, segment, block_size, score_scale
    )
    returned = lax.all_to_all(
        heads_out.reshape(length_total, 1, group_width),
        "seq",
        split_axis=0,
        concat_axis=1,
        tiled=True,
    )
    attn_rows = returned.reshape(row_count, model_width)
    resid = tokens_in + jnp.dot(attn_rows, full_out, preferred_element_type=jnp.float32)
    normed_two, inv_std_two = norm_parts(resid)
    hidden_two = (normed_two * gain_two + shift_two.astype(jnp.float32)).astype(jnp.bfloat16)
    piece_gate = lax.all_gather(w_gate_up, "fsdp", axis=0, tiled=True)
    piece_down = lax.all_gather(w_down, "fsdp", axis=0, tiled=True)
    gate_up = jnp.einsum("td,ukd->tku", hidden_two, piece_gate, preferred_element_type=jnp.float32)
    hidden_piece = (jax.nn.silu(gate_up[:, 0]) * gate_up[:, 1]).astype(jnp.bfloat16)
    running = jnp.dot(hidden_piece, piece_down, preferred_element_type=jnp.float32)
    outputs = resid + running
    differ = outputs - teacher_in
    cot = counted[:, None] * differ
    half_sum = 0.5 * jnp.sum(cot * differ)
    count_here = jnp.sum(counted)
    cot_low = cot.astype(jnp.bfloat16)
    piece_gate = lax.all_gather(w_gate_up, "fsdp", axis=0, tiled=True)
    piece_down = lax.all_gather(w_down, "fsdp", axis=0, tiled=True)
    hidden_grad = jnp.einsum("tc,uc->tu", cot_low, piece_down, preferred_element_type=jnp.float32)
    piece_grads = gate_backward(gate_up, hidden_grad)
    grad_running = jnp.einsum(
        "tku,ukd->td", piece_grads, piece_gate, preferred_element_type=jnp.float32
    )

    def unit_rows(first_row, row_total):
        gate_term = jnp.einsum(
            "tku,td->ukd", piece_grads, hidden_two, preferred_element_type=jnp.float32
        )
        down_term = jnp.einsum(
            "tu,td->ud", hidden_piece, cot_low, preferred_element_type=jnp.float32
        )
        return jnp.concatenate([gate_term, down_term[:, None]], axis=1)

    ff_shard = reduce_rows(unit_rows, w_down.shape[0])
    resid_grad = cot + norm_back(grad_running, normed_two, inv_std_two, gain_two)
    gain_two_grad = jnp.sum(grad_running * normed_two, axis=0)
    shift_two_grad = jnp.sum(grad_running, axis=0)
    resid_low = resid_grad.astype(jnp.bfloat16)
    out_grad = jnp.einsum(
        "tc,ec->te", resid_low, full_out, preferred_element_type=jnp.float32
    ).astype(jnp.bfloat16)
    head_grad = lax.all_to_all(
        out_grad.reshape(row_count, seq_count, group_width),
        "seq",
        split_axis=1,
        concat_axis=0,
        tiled=True,
    )
    head_grad = head_grad.reshape(length_total, heads_here, HD)
    query_grad, key_grad, value_grad = attention_backward(
        query_rows, key_rows, value_rows, head_grad, log_totals, segment, block_size, score_scale
    )
    back_packed = jnp.stack(
        [
            rotate(query_grad, positions_all, -1.0),
            rotate(key_grad, positions_all, -1.0),
            value_grad,
        ],
        axis=1,
    )
    back_packed = back_packed.astype(jnp.bfloat16).reshape(length_total, 3, 1, group_width)
    qkv_grad = lax.all_to_all(back_packed, "seq", split_axis=0, concat_axis=2, tiled=True).reshape(
        row_count, 3 * model_width
    )
    grad_one = jnp.einsum("tc,ec->te", qkv_grad, full_qkv, preferred_element_type=jnp.float32)
    tokens_grad = resid_grad + norm_back(grad_one, normed_one, inv_std_one, gain_one)
    gain_one_grad = jnp.sum(grad_one * normed_one, axis=0)
    shift_one_grad = jnp.sum(grad_one, axis=0)
    bias_grad = jnp.sum(qkv_grad.astype(jnp.float32), axis=0)

    def feature_rows(first_row, row_total):
        qkv_term = jnp.einsum("tr,tc->rc", hidden_one, qkv_grad, preferred_element_type=jnp.float32)
        out_term = jnp.einsum("tr,tc->rc", attn_rows, resid_low, preferred_element_type=jnp.float32)
        return jnp.concatenate([qkv_term, out_term], axis=1)

    attn_shard = reduce_rows(feature_rows, w_qkv.shape[0])
    attn_total, ff_total = (
        lax.psum(attn_shard.astype(jnp.bfloat16), "seq").astype(jnp.float32),
        lax.psum(ff_shard.astype(jnp.bfloat16), "seq").astype(jnp.float32),
    )
    (
        sum_half,
        sum_count,
        total_gain_one,
        total_shift_one,
        total_gain_two,
        total_shift_two,
        total_bias,
    ) = lax.psum(
        (
            half_sum,
            count_here,
            gain_one_grad,
            shift_one_grad,
            gain_two_grad,
            shift_two_grad,
            bias_grad,
        ),
        ("seq", "fsdp"),
    )
    factor = tokens_total / sum_count
    loss = 2.0 * sum_half / (sum_count * model_width)

    def own_part(total_vec):
        share = total_vec.shape[0] // fsdp_count
        return factor * lax.dynamic_slice_in_dim(total_vec, fsdp_index * share, share, 0)

    layer_out = outputs.astype(jnp.bfloat16)[None]
    grad_tokens = (factor * tokens_grad).astype(jnp.bfloat16)[None]
    return (
        layer_out,
        loss,
        grad_tokens,
        own_part(total_gain_one),
        own_part(total_shift_one),
        factor * attn_total[:, : 3 * model_width],
        own_part(total_bias),
        factor * attn_total[:, 3 * model_width :],
        own_part(total_gain_two),
        own_part(total_shift_two),
        factor * ff_total[:, :2],
        factor * ff_total[:, 2],
    )


def solution(mesh):
    placed = (
        P("fsdp", "seq", None),
        P("fsdp", "seq", None),
        P("fsdp", None),
        P("fsdp", "seq"),
        P("fsdp"),
        P("fsdp"),
        P("fsdp", None),
        P("fsdp"),
        P("fsdp", None),
        P("fsdp"),
        P("fsdp"),
        P("fsdp", None, None),
        P("fsdp", None),
    )
    return jax.shard_map(
        per_device,
        mesh=mesh,
        in_specs=placed,
        out_specs=(
            P("fsdp", "seq", None),
            P(),
            P("fsdp", "seq", None),
            P("fsdp"),
            P("fsdp"),
            P("fsdp", None),
            P("fsdp"),
            P("fsdp", None),
            P("fsdp"),
            P("fsdp"),
            P("fsdp", None, None),
            P("fsdp", None),
        ),
        check_vma=False,
    )
```

profile of v0, /device:TPU:0, one launch (start us, length us, event | category | flops | bytes accessed | tf_op | source)
XLA Modules:
  0.0 4082.9 jit_solution(5188963605835579992)
XLA Ops:
  17.8 48.8 %all-gather.1 = bf16[8,1,256]{2,1,0:T(2,128)(2,1)S(1)} all-gather(bf16[1,1,256]{2,1,0:T(2,128)(2,1)S(1)} %reshape.465), channel_id=1, replica_groups=mesh['seq'=4,'fsdp'=8] {'fsdp'}, dimensions={0}, use_global_device_ids=true | all-gather | bytes 4608 | tf_op jit(solution)/shard_map/all_gather | solution.py:180
  66.6 30.9 all-gather
  97.5 39.9 all-gather.2
  139.2 354.2 %all-gather.10.cloned.1.call-done = bf16[2048,6144]{1,0:T(8,128)(2,1)} async-done(((bf16[256,6144]{1,0:T(8,128)(2,1)}), bf16[2048,6144]{1,0:T(8,128)(2,1)}) %all-gather.10.cloned.1.call-update) | async-done | bytes 25165840 | tf_op jit(solution)/shard_map/all_gather | solution.py:176
  524.5 36.8 all-to-all-done
  575.3 37.4 while.27
  638.5 64.3 %all-gather.4 = bf16[8,1,256]{2,1,0:T(2,128)(2,1)S(1)} all-gather(bf16[1,1,256]{2,1,0:T(2,128)(2,1)S(1)} %reshape.471), channel_id=1, replica_groups=mesh['seq'=4,'fsdp'=8] {'fsdp'}, dimensions={0}, use_global_device_ids=true | all-gather | bytes 4608 | tf_op jit(solution)/shard_map/all_gather | solution.py:182
  702.8 30.6 all-gather.3
  745.9 748.3 %all-gather.14.cloned.1.call-done = bf16[5632,2,2048]{2,0,1:T(8,128)(2,1)} async-done(((bf16[704,2,2048]{2,0,1:T(8,128)(2,1)}), bf16[5632,2,2048]{2,0,1:T(8,128)(2,1)}) %all-gather.14.cloned.1.call-update) | async-done | bytes 46137360 | tf_op jit(solution)/shard_map/all_gather | solution.py:226
  1494.3 23.7 convolution_bitcast_fusion
  1524.3 412.4 %all-gather.16.cloned.1.call-done = bf16[5632,2048]{1,0:T(8,128)(2,1)} async-done(((bf16[704,2048]{1,0:T(8,128)(2,1)}), bf16[5632,2048]{1,0:T(8,128)(2,1)}) %all-gather.16.cloned.1.call-update) | async-done | bytes 23068688 | tf_op jit(solution)/shard_map/all_gather | solution.py:227
  1961.9 25.6 fusion.31
  1987.4 21.2 convert_bitcast_fusion
  2008.6 46.8 %pad_maximum_fusion = bf16[5632,3,2048]{0,2,1:T(8,128)(2,1)} fusion(bf16[5632,1,2048]{0,2,1:T(8,128)(2,1)} %convert_bitcast_fusion.1, bf16[5632,2,2048]{0,2,1:T(8,128)(2,1)} %convert_bitcast_fusion), kind=kLoop, calls=%fused_computation.40 | loop fusion | flops 34603008 | bytes 138412032 | tf_op jit(solution)/shard_map/concatenate | solution.py:252
  2055.4 88.8 %copy.142 = bf16[5632,6144]{1,0:T(8,128)(2,1)} copy(bf16[5632,6144]{0,1:T(8,128)(2,1)} %bitcast.64) | data formatting | bytes 138412032
  2144.3 22.0 multiply_reduce_fusion.1
  2197.4 154.1 %while.28 = (s32[]{:T(128)}, f32[1024,8,64]{0,2,1:T(8,128)}, f32[1024,8,64]{0,2,1:T(8,128)}, f32[2,512,8,64]{1,0,3,2:T(2,128)}, s32[2]{0:T(128)S(1)}, /*index=5*...) while((s32[]{:T(128)}, f32[1024,8,64]{0,2,1:T(8,128)}, ...), condition=%wide.region_18.19_spmd.clone, body=%wide.region_16.18_spmd.clone.sunk | while | flops 2726556160 | bytes 233929072 | solution.py:133
  2254.5 19.7 dynamic_update_slice.20
  2376.5 42.4 %all-to-all-done.3 = bf16[1024,3,1,512]{3,1,2,0:T(4,128)(2,1)} async-done(((bf16[1024,3,1,512]{3,1,2,0:T(4,128)(2,1)}), bf16[1024,3,1,512]{3,1,2,0:T(4,128)(2,1)}, u32[]{:S(2)}, u32[]{:S(2)}) %all-to-all-start.3) | async-done | bytes 3145760 | tf_op jit(solution)/shard_map/all_to_all | solution.py:282
  2442.9 22.9 pad_maximum_fusion.1
  2465.8 764.0 %reduce-scatter.7.cloned.1.call-done = bf16[704,6144]{1,0:T(8,128)(2,1)} async-done(((bf16[5632,6144]{1,0:T(8,128)(2,1)}), bf16[704,6144]{1,0:T(8,128)(2,1)}) %reduce-scatter.7.cloned.1.call-update) | async-done | bytes 8650768
  3242.6 529.5 %reduce-scatter.5.cloned.1.call-done = bf16[256,8192]{1,0:T(8,128)(2,1)} async-done(((bf16[2048,8192]{1,0:T(8,128)(2,1)}), bf16[256,8192]{1,0:T(8,128)(2,1)}) %reduce-scatter.5.cloned.1.call-update) | async-done | bytes 4194320 | tf_op jit(solution)/shard_map/reduce_scatter | solution.py:140
  3791.6 41.5 %all-reduce = (f32[]{:T(128)}, f32[]{:T(128)}, f32[2048]{0:T(1024)S(1)}, f32[2048]{0:T(1024)S(1)}, f32[6144]{0:T(1024)S(1)}, /*index=5*/f32[2048]{0:T(1024)S(1)}, f32[2048]{0:T(1024)S(1)}) all-reduce(f32[]{:T(128)S(6)} %mul_shard_map.3, f32[]{:T(128)} %convert_reduce_fusion.2, ...), channel_id=1, replica_groups=mesh['seq'=4,'fsdp'=8] {'seq','fsdp'}, use_global_device_ids=true, to_apply=%region_11.12 | all-reduce | flops 14338 | bytes 114704 | tf_op jit(solution)/shard_map/psum | solution.py:309
  3841.8 171.7 %all-reduce.4.cloned.1.call-done = (bf16[256,8192]{1,0:T(8,128)(2,1)}, bf16[704,3,2048]{0,2,1:T(8,128)(2,1)}) async-done(((bf16[256,8192]{1,0:T(8,128)(2,1)}, bf16[704,3,2048]{0,2,1:T(8,128)(2,1)}), (bf16[256,8192]{1,0:T(8,128)(2,1)}, bf16[704,3,2048]{0,2,1:T(8,128)(2,1)})) %all-reduce.4.cloned.1.call-update) | async-done | bytes 12845072 | tf_op jit(solution)/shard_map/psum | solution.py:298
  (268 shorter events, 469.5 us)
Async XLA Ops:
  7.2 486.2 %all-gather.10.cloned.1.call-start = ((), (), s32[]{:S(2)}) async-start(), calls=%async_computation.6 | async-start | bytes 28311552 | tf_op jit(solution)/shard_map/all_gather | solution.py:176
  7.9 731.3 %all-gather.12.cloned.1.call-start = ((), (), s32[]{:S(2)}) async-start(), calls=%async_computation.7 | async-start | bytes 9437184 | tf_op jit(solution)/shard_map/all_gather | solution.py:177
  8.7 1485.6 %all-gather.14.cloned.1.call-start = ((), (), s32[]{:S(2)}) async-start(), calls=%async_computation.8 | async-start | bytes 51904512 | tf_op jit(solution)/shard_map/all_gather | solution.py:226
  16.5 121.9 %copy-start.8 = (bf16[1,256,2048]{2,1,0:T(8,128)(2,1)S(1)}, bf16[1,256,2048]{2,1,0:T(8,128)(2,1)}, u32[]{:S(2)}) copy-start(bf16[1,256,2048]{2,1,0:T(8,128)(2,1)} %param.17) | copy-start | bytes 3145732
  16.6 1920.1 %all-gather.16.cloned.1.call-start = ((), (), s32[]{:S(2)}) async-start(), calls=%async_computation.9 | async-start | bytes 25952256 | tf_op jit(solution)/shard_map/all_gather | solution.py:227
  66.6 440.2 %copy-start.22 = (f32[8,1,256]{2,1,0:T(1,128)}, f32[8,1,256]{2,1,0:T(1,128)S(1)}, u32[]{:S(2)}) copy-start(f32[8,1,256]{2,1,0:T(1,128)S(1)} %convert_element_type.149) | copy-start | bytes 24580
  97.5 409.3 %copy-start.20 = (f32[8,1,256]{2,1,0:T(1,128)}, f32[8,1,256]{2,1,0:T(1,128)S(1)}, u32[]{:S(2)}) copy-start(f32[8,1,256]{2,1,0:T(1,128)S(1)} %convert_element_type.148) | copy-start | bytes 24580
  137.5 369.3 %copy-start.37 = (f32[8]{0:T(128)}, f32[8]{0:T(128)S(1)}, u32[]{:S(2)}) copy-start(f32[8]{0:T(128)S(1)} %multiply_power_fusion) | copy-start | bytes 100
  138.6 368.2 %copy-start.28 = (f32[256]{0:T(256)}, f32[256]{0:T(256)S(1)}, u32[]{:S(2)}) copy-start(f32[256]{0:T(256)S(1)} %broadcast_multiply_fusion.5) | copy-start | bytes 3076
  139.0 367.8 %copy-start.30 = (f32[256]{0:T(256)}, f32[256]{0:T(256)S(1)}, u32[]{:S(2)}) copy-start(f32[256]{0:T(256)S(1)} %add_rsqrt_fusion.1) | copy-start | bytes 3076
  520.6 40.8 all-to-all-start
  612.8 125.1 %copy-start.1 = (bf16[1024,8,64]{0,2,1:T(8,128)(2,1)}, bf16[1024,8,64]{0,2,1:T(8,128)(2,1)S(1)}, u32[]{:S(2)}) copy-start(bf16[1024,8,64]{0,2,1:T(8,128)(2,1)S(1)} %get-tuple-element.590) | copy-start | bytes 3145732
  634.8 98.6 %all-to-all-start.1 = ((bf16[4,2,65536]{2,1,0:T(2,128)(2,1)}), bf16[4,2,65536]{2,1,0:T(2,128)(2,1)S(1)}, u32[]{:S(2)}, u32[]{:S(2)}) async-start(bf16[4,2,65536]{2,1,0:T(2,128)(2,1)} %reshape.486), calls=%async_computation.1 | async-start | bytes 2097152 | tf_op jit(solution)/shard_map/all_to_all | solution.py:215
  638.4 2591.4 %reduce-scatter.7.cloned.1.call-start = ((), (), s32[]{:S(2)}) async-start(), calls=%async_computation.11 | async-start | bytes 77856768
  638.5 1298.2 %copy-start.35 = (f32[1,256]{1,0:T(1,128)}, f32[1,256]{1,0:T(1,128)S(1)}, u32[]{:S(2)}) copy-start(f32[1,256]{1,0:T(1,128)S(1)} %convert_element_type.133) | copy-start | bytes 3076
  1518.0 418.7 %copy-start.17 = (bf16[1,256,2048]{2,1,0:T(8,128)(2,1)S(1)}, bf16[1,256,2048]{2,1,0:T(8,128)(2,1)}, u32[]{:S(2)}) copy-start(bf16[1,256,2048]{2,1,0:T(8,128)(2,1)} %param.18) | copy-start | bytes 3145732
  2144.2 22.0 copy-start.14
  2144.2 22.0 copy-start.18
  2144.3 22.0 copy-start.36
  2177.1 18.1 all-to-all-start.2
  2253.4 20.7 copy-start.3
  2365.6 53.3 %all-to-all-start.3 = ((bf16[1024,3,1,512]{3,1,2,0:T(4,128)(2,1)}), bf16[1024,3,1,512]{3,1,2,0:T(4,128)(2,1)}, u32[]{:S(2)}, u32[]{:S(2)}) async-start(bf16[1024,3,1,512]{3,1,2,0:T(4,128)(2,1)} %copy.126), calls=%async_computation.3 | async-start | bytes 8388608 | tf_op jit(solution)/shard_map/all_to_all | solution.py:282
  2370.7 1401.4 %reduce-scatter.5.cloned.1.call-start = ((), (), s32[]{:S(2)}) async-start(), calls=%async_computation.10 | async-start | bytes 37748736 | tf_op jit(solution)/shard_map/reduce_scatter | solution.py:140
  2465.8 1547.7 %all-reduce.4.cloned.1.call-start = ((), (), s32[]{:S(2)}) async-start(), calls=%async_computation.12 | async-start | bytes 27262976 | tf_op jit(solution)/shard_map/psum | solution.py:298
  (39 other events, 313.1 us)
Sparse Core Ops, SparseCore 0:
  9.5 483.8 all-gather.9
  495.5 124.4 all-gather.11
  622.1 872.0 all-gather.13
  1495.6 441.0 all-gather.15
  2144.4 1085.4 reduce-scatter.6
  3233.5 538.6 reduce-scatter.4
  3775.3 238.1 all-reduce.3
where the time goes:
time: 4100 us; the launch traced here: 4080 us
  waiting for transfers between devices  3070 us (75%)
  matrix products  270 us (7%)
  local copies, waits for them, and re-layouts  262 us (6%)
  blocking collectives  256 us (6%)
  other arithmetic  175 us (4%)
    unnamed x8, waiting for transfers between devices  766 us
    all_gather x1, waiting for transfers between devices, per_device(): piece_gate = lax.all_gather(w_gate_up, 'fsdp', axis=0, tiled=True)  748 us
    reduce_scatter x1, waiting for transfers between devices, reduce_rows(): lax.psum_scatter(term_rows(jnp.int32(0), row_share * lax.axis_size('fsdp'...  530 us
    all_gather x1, waiting for transfers between devices, per_device(): piece_down = lax.all_gather(w_down, 'fsdp', axis=0, tiled=True)  412 us
    all_gather x1, waiting for transfers between devices, per_device(): lax.all_gather(w_qkv, 'fsdp', axis=0, tiled=True)  354 us
    psum x1, waiting for transfers between devices, per_device(): lax.psum(attn_shard.astype(jnp.bfloat16), 'seq').astype(jnp.float32)  172 us
    unnamed x102, local copies, waits for them, and re-layouts  144 us
  transfers between devices with their start and end apart: 11, of which 9 were waited for; matrix products, arithmetic and copies ran while one was open for 10% of the time, Pallas kernels for 0%

commit v1 on v0

--- a/solution.py
+++ b/solution.py
@@ -8,6 +8,24 @@
 ROT = 16
 EPSILON = 1e-05
 MASKED_VALUE = -1e30
+
+
+def collect(shard, axis, dim):
+    ways, here, turn = (lax.axis_size(axis), lax.axis_index(axis), shard.shape[dim])
+    dims = [n * ways if d == dim else n for d, n in enumerate(shard.shape)]
+    full = lax.dynamic_update_slice_in_dim(
+        jnp.zeros(dims, shard.dtype), shard, here * turn, axis=dim
+    )
+    going_up = going_down = shard
+    for far in range(1, ways // 2 + 1):
+        going_up = lax.ppermute(going_up, axis, [(d, (d + 1) % ways) for d in range(ways)])
+        full = lax.dynamic_update_slice_in_dim(full, going_up, (here - far) % ways * turn, axis=dim)
+        if 2 * far < ways:
+            going_down = lax.ppermute(going_down, axis, [(d, (d - 1) % ways) for d in range(ways)])
+            full = lax.dynamic_update_slice_in_dim(
+                full, going_down, (here + far) % ways * turn, axis=dim
+            )
+    return full
 
 
 def norm_parts(values):
@@ -224,7 +242,7 @@
     normed_two, inv_std_two = norm_parts(resid)
     hidden_two = (normed_two * gain_two + shift_two.astype(jnp.float32)).astype(jnp.bfloat16)
     piece_gate = lax.all_gather(w_gate_up, "fsdp", axis=0, tiled=True)
-    piece_down = lax.all_gather(w_down, "fsdp", axis=0, tiled=True)
+    piece_down = collect(w_down, "fsdp", 0)
     gate_up = jnp.einsum("td,ukd->tku", hidden_two, piece_gate, preferred_element_type=jnp.float32)
     hidden_piece = (jax.nn.silu(gate_up[:, 0]) * gate_up[:, 1]).astype(jnp.bfloat16)
     running = jnp.dot(hidden_piece, piece_down, preferred_element_type=jnp.float32)

time: 4100 us -> 4480 us (1.093)
  blocking collectives: 256 us -> 458 us
  waiting for transfers between devices: 3070 us -> 3200 us
    ppermute x0 -> x7, waiting for transfers between devices: none -> 395 us  [the longest x4 274 us: collect(): lax.ppermute(going_up, axis, [(d, (d + 1) % ways) for d in range(ways)])]
    all_gather x1, waiting for transfers between devices: 354 us -> 135 us  [per_device(): lax.all_gather(w_qkv, 'fsdp', axis=0, tiled=True)]
    all_gather x1, blocking collectives: 39.9 us -> 199 us  [per_device(): lax.all_gather(b_qkv, 'fsdp', axis=0, tiled=True)]
    all_gather x1, blocking collectives: 30.9 us -> 83.4 us  [per_device(): lax.all_gather(ln1_gain, 'fsdp', axis=0, tiled=True)]
    all_gather x1, blocking collectives: 64.3 us -> 18.3 us  [per_device(): lax.all_gather(ln2_bias, 'fsdp', axis=0, tiled=True)]
    unnamed x102 -> x110, local copies, waits for them, and re-layouts: 144 us -> 143 us
  transfers between devices with their start and end apart: 11 -> 18, of which waited for: 9 -> 10; matrix products, arithmetic and copies ran while one was open for 10% -> 11% of each run, Pallas kernels for 0% -> 0%
where the time goes in v1:
time: 4480 us; the launch traced here: 4470 us
  waiting for transfers between devices  3200 us (71%)
  blocking collectives  458 us (10%)
  local copies, waits for them, and re-layouts  292 us (7%)
  matrix products  272 us (6%)
  other arithmetic  186 us (4%)
    all_gather x1, waiting for transfers between devices, per_device(): piece_gate = lax.all_gather(w_gate_up, 'fsdp', axis=0, tiled=True)  774 us
    unnamed x8, waiting for transfers between devices  754 us
    reduce_scatter x1, waiting for transfers between devices, reduce_rows(): lax.psum_scatter(term_rows(jnp.int32(0), row_share * lax.axis_size('fsdp'...  530 us
    all_gather x1, waiting for transfers between devices, per_device(): piece_down = lax.all_gather(w_down, 'fsdp', axis=0, tiled=True)  386 us
    ppermute x4, waiting for transfers between devices, collect(): lax.ppermute(going_up, axis, [(d, (d + 1) % ways) for d in range(ways)])  274 us
    all_gather x1, blocking collectives, per_device(): lax.all_gather(b_qkv, 'fsdp', axis=0, tiled=True)  199 us
    psum x1, waiting for transfers between devices, per_device(): lax.psum(attn_shard.astype(jnp.bfloat16), 'seq').astype(jnp.float32)  172 us
    unnamed x110, local copies, waits for them, and re-layouts  143 us
  transfers between devices with their start and end apart: 18, of which 10 were waited for; matrix products, arithmetic and copies ran while one was open for 11% of the time, Pallas kernels for 0%

profile of v1, /device:TPU:0, one launch (start us, length us, event | category | flops | bytes accessed | tf_op | source)
XLA Modules:
  0.0 4466.8 jit_solution(9015921665729905570)
XLA Ops:
  23.3 274.3 %collective-permute-done = bf16[704,2048]{1,0:T(8,128)(2,1)} collective-permute-done((bf16[704,2048]{1,0:T(8,128)(2,1)}, bf16[704,2048]{1,0:T(8,128)(2,1)}, u32[]{:S(2)}, u32[]{:S(2)}) %collective-permute-start) | collective-permute-done | bytes 2883616 | tf_op jit(solution)/shard_map/ppermute | solution.py:21
  300.1 199.3 %all-gather.2 = bf16[8,1,768]{2,1,0:T(2,128)(2,1)S(1)} all-gather(bf16[1,1,768]{2,1,0:T(2,128)(2,1)S(1)} %reshape.467), channel_id=1, replica_groups=mesh['seq'=4,'fsdp'=8] {'fsdp'}, dimensions={0}, use_global_device_ids=true | all-gather | bytes 13824 | tf_op jit(solution)/shard_map/all_gather | solution.py:196
  499.4 85.1 %all-gather.1 = bf16[8,1,256]{2,1,0:T(2,128)(2,1)S(1)} all-gather(bf16[1,1,256]{2,1,0:T(2,128)(2,1)S(1)} %reshape.465), channel_id=1, replica_groups=mesh['seq'=4,'fsdp'=8] {'fsdp'}, dimensions={0}, use_global_device_ids=true | all-gather | bytes 4608 | tf_op jit(solution)/shard_map/all_gather | solution.py:198
  584.6 83.4 %all-gather = bf16[8,1,256]{2,1,0:T(2,128)(2,1)S(1)} all-gather(bf16[1,1,256]{2,1,0:T(2,128)(2,1)S(1)} %reshape.463), channel_id=1, replica_groups=mesh['seq'=4,'fsdp'=8] {'fsdp'}, dimensions={0}, use_global_device_ids=true | all-gather | bytes 4608 | tf_op jit(solution)/shard_map/all_gather | solution.py:197
  672.4 135.3 %all-gather.10.cloned.1.call-done = bf16[2048,6144]{1,0:T(8,128)(2,1)} async-done(((bf16[256,6144]{1,0:T(8,128)(2,1)}), bf16[2048,6144]{1,0:T(8,128)(2,1)}) %all-gather.10.cloned.1.call-update) | async-done | bytes 25165840 | tf_op jit(solution)/shard_map/all_gather | solution.py:194
  839.0 30.6 all-gather.3
  930.8 37.4 while.27
  997.5 121.1 %collective-permute-done.5 = bf16[704,2048]{1,0:T(8,128)(2,1)} collective-permute-done((bf16[704,2048]{1,0:T(8,128)(2,1)}, bf16[704,2048]{1,0:T(8,128)(2,1)}, u32[]{:S(2)}, u32[]{:S(2)}) %collective-permute-start.5) | collective-permute-done | bytes 2883616 | tf_op jit(solution)/shard_map/ppermute | solution.py:24
  1137.4 774.5 %all-gather.14.cloned.1.call-done = bf16[5632,2,2048]{2,0,1:T(8,128)(2,1)} async-done(((bf16[704,2,2048]{2,0,1:T(8,128)(2,1)}), bf16[5632,2,2048]{2,0,1:T(8,128)(2,1)}) %all-gather.14.cloned.1.call-update) | async-done | bytes 46137360 | tf_op jit(solution)/shard_map/all_gather | solution.py:244
  1911.8 23.7 convolution_bitcast_fusion
  1968.2 386.1 %all-gather.16.cloned.1.call-done = bf16[5632,2048]{1,0:T(8,128)(2,1)} async-done(((bf16[704,2048]{1,0:T(8,128)(2,1)}), bf16[5632,2048]{1,0:T(8,128)(2,1)}) %all-gather.16.cloned.1.call-update) | async-done | bytes 23068688 | tf_op jit(solution)/shard_map/all_gather | solution.py:256
  2372.0 21.2 convert_bitcast_fusion
  2393.2 46.3 %pad_maximum_fusion = bf16[5632,3,2048]{0,2,1:T(8,128)(2,1)} fusion(bf16[5632,1,2048]{0,2,1:T(8,128)(2,1)} %convert_bitcast_fusion.1, bf16[5632,2,2048]{0,2,1:T(8,128)(2,1)} %convert_bitcast_fusion), kind=kLoop, calls=%fused_computation.40 | loop fusion | flops 34603008 | bytes 138412032 | tf_op jit(solution)/shard_map/concatenate | solution.py:270
  2439.6 88.8 %copy.142 = bf16[5632,6144]{1,0:T(8,128)(2,1)} copy(bf16[5632,6144]{0,1:T(8,128)(2,1)} %bitcast.64) | data formatting | bytes 138412032
  2528.4 22.0 multiply_reduce_fusion.1
  2581.6 164.2 %while.28 = (s32[]{:T(128)}, f32[1024,8,64]{0,2,1:T(8,128)}, f32[1024,8,64]{0,2,1:T(8,128)}, f32[2,512,8,64]{1,0,3,2:T(2,128)}, s32[2]{0:T(128)S(1)}, /*index=5*...) while((s32[]{:T(128)}, f32[1024,8,64]{0,2,1:T(8,128)}, ...), condition=%wide.region_18.19_spmd.clone, body=%wide.region_16.18_spmd.clone.sunk | while | flops 2726556160 | bytes 242317680 | solution.py:151
  2643.2 19.6 dynamic_update_slice.60
  2726.0 19.6 dynamic_update_slice.60
  2772.0 42.4 all-to-all-done.3
  2838.1 23.6 pad_maximum_fusion.1
  2861.8 751.9 %reduce-scatter.7.cloned.1.call-done = bf16[704,6144]{1,0:T(8,128)(2,1)} async-done(((bf16[5632,6144]{1,0:T(8,128)(2,1)}), bf16[704,6144]{1,0:T(8,128)(2,1)}) %reduce-scatter.7.cloned.1.call-update) | async-done | bytes 8650768
  3626.5 529.7 %reduce-scatter.5.cloned.1.call-done = bf16[256,8192]{1,0:T(8,128)(2,1)} async-done(((bf16[2048,8192]{1,0:T(8,128)(2,1)}), bf16[256,8192]{1,0:T(8,128)(2,1)}) %reduce-scatter.5.cloned.1.call-update) | async-done | bytes 4194320 | tf_op jit(solution)/shard_map/reduce_scatter | solution.py:158
  4175.6 41.4 all-reduce
  4225.8 171.7 %all-reduce.4.cloned.1.call-done = (bf16[256,8192]{1,0:T(8,128)(2,1)}, bf16[704,3,2048]{0,2,1:T(8,128)(2,1)}) async-done(((bf16[256,8192]{1,0:T(8,128)(2,1)}, bf16[704,3,2048]{0,2,1:T(8,128)(2,1)}), (bf16[256,8192]{1,0:T(8,128)(2,1)}, bf16[704,3,2048]{0,2,1:T(8,128)(2,1)})) %all-reduce.4.cloned.1.call-update) | async-done | bytes 12845072 | tf_op jit(solution)/shard_map/psum | solution.py:316
  (301 shorter events, 547.4 us)
Async XLA Ops:
  7.2 800.6 %all-gather.10.cloned.1.call-start = ((), (), s32[]{:S(2)}) async-start(), calls=%async_computation.6 | async-start | bytes 28311552 | tf_op jit(solution)/shard_map/all_gather | solution.py:194
  7.9 1122.8 %all-gather.12.cloned.1.call-start = ((), (), s32[]{:S(2)}) async-start(), calls=%async_computation.7 | async-start | bytes 9437184 | tf_op jit(solution)/shard_map/all_gather | solution.py:195
  8.7 1903.2 %all-gather.14.cloned.1.call-start = ((), (), s32[]{:S(2)}) async-start(), calls=%async_computation.8 | async-start | bytes 51904512 | tf_op jit(solution)/shard_map/all_gather | solution.py:244
  16.5 482.9 %copy-start.44 = (bf16[256]{0:T(256)(128)(2,1)S(1)}, bf16[256]{0:T(256)(128)(2,1)}, u32[]{:S(2)}) copy-start(bf16[256]{0:T(256)(128)(2,1)} %param.22) | copy-start | bytes 1540
  16.5 568.1 %copy-start.45 = (bf16[256]{0:T(256)(128)(2,1)S(1)}, bf16[256]{0:T(256)(128)(2,1)}, u32[]{:S(2)}) copy-start(bf16[256]{0:T(256)(128)(2,1)} %param.21) | copy-start | bytes 1540
  16.5 651.6 %copy-start.16 = (s32[1,1024]{1,0:T(1,128)S(1)}, s32[1,1024]{1,0:T(1,128)}, u32[]{:S(2)}) copy-start(s32[1,1024]{1,0:T(1,128)} %param.19) | copy-start | bytes 12292
  16.5 653.0 %copy-start.4 = (bf16[1,256,2048]{2,1,0:T(8,128)(2,1)S(1)}, bf16[1,256,2048]{2,1,0:T(8,128)(2,1)}, u32[]{:S(2)}) copy-start(bf16[1,256,2048]{2,1,0:T(8,128)(2,1)} %param.17) | copy-start | bytes 3145732
  16.6 2337.8 %all-gather.16.cloned.1.call-start = ((), (), s32[]{:S(2)}) async-start(), calls=%async_computation.9 | async-start | bytes 25952256 | tf_op jit(solution)/shard_map/all_gather | solution.py:256
  17.1 280.5 %collective-permute-start = (bf16[704,2048]{1,0:T(8,128)(2,1)}, bf16[704,2048]{1,0:T(8,128)(2,1)}, u32[]{:S(2)}, u32[]{:S(2)}) collective-permute-start(bf16[704,2048]{1,0:T(8,128)(2,1)} %param.29), channel_id=1, source_target_pairs={{0,1},{1,2},{2,3},{3,4},{4,5},{5,6},{6,7},{7,0},{8,9},{9,10},{10,1... | collective-permute-start | bytes 8650760 | tf_op jit(solution)/shard_map/ppermute | solution.py:21
  20.2 650.2 %collective-permute-start.1 = (bf16[704,2048]{1,0:T(8,128)(2,1)}, bf16[704,2048]{1,0:T(8,128)(2,1)}, u32[]{:S(2)}, u32[]{:S(2)}) collective-permute-start(bf16[704,2048]{1,0:T(8,128)(2,1)} %param.29), channel_id=1, source_target_pairs={{0,7},{1,0},{2,1},{3,2},{4,3},{5,4},{6,5},{7,6},{8,15},{9,8},{10,9... | collective-permute-start | bytes 8650760 | tf_op jit(solution)/shard_map/ppermute | solution.py:24
  297.6 372.8 %collective-permute-start.2 = (bf16[704,2048]{1,0:T(8,128)(2,1)}, bf16[704,2048]{1,0:T(8,128)(2,1)}, u32[]{:S(2)}, u32[]{:S(2)}) collective-permute-start(bf16[704,2048]{1,0:T(8,128)(2,1)} %collective-permute-done), channel_id=1, source_target_pairs={{0,1},{1,2},{2,3},{3,4},{4,5},{5,6},{6,7},{7,0},{8,9},{9,10},{10,1... | collective-permute-start | bytes 8650760 | tf_op jit(solution)/shard_map/ppermute | solution.py:21
  670.4 236.8 %collective-permute-start.3 = (bf16[704,2048]{1,0:T(8,128)(2,1)}, bf16[704,2048]{1,0:T(8,128)(2,1)}, u32[]{:S(2)}, u32[]{:S(2)}) collective-permute-start(bf16[704,2048]{1,0:T(8,128)(2,1)} %collective-permute-done.1), channel_id=1, source_target_pairs={{0,7},{1,0},{2,1},{3,2},{4,3},{5,4},{6,5},{7,6},{8,15},{9,8},{10,9... | collective-permute-start | bytes 8650760 | tf_op jit(solution)/shard_map/ppermute | solution.py:24
  670.4 244.8 %collective-permute-start.4 = (bf16[704,2048]{1,0:T(8,128)(2,1)}, bf16[704,2048]{1,0:T(8,128)(2,1)}, u32[]{:S(2)}, u32[]{:S(2)}) collective-permute-start(bf16[704,2048]{1,0:T(8,128)(2,1)} %collective-permute-done.2), channel_id=1, source_target_pairs={{0,1},{1,2},{2,3},{3,4},{4,5},{5,6},{6,7},{7,0},{8,9},{9,10},{10,1... | collective-permute-start | bytes 8650760 | tf_op jit(solution)/shard_map/ppermute | solution.py:21
  835.0 81.8 %all-to-all-start = ((bf16[256,3,4,512]{0,3,1,2:T(8,128)(2,1)}), bf16[256,3,4,512]{0,3,1,2:T(8,128)(2,1)S(1)}, u32[]{:S(2)}, u32[]{:S(2)}) async-start(bf16[256,3,4,512]{0,3,1,2:T(8,128)(2,1)} %copy.117), calls=%async_computation | async-start | bytes 6291456 | tf_op jit(solution)/shard_map/all_to_all | solution.py:225
  907.1 211.4 %collective-permute-start.5 = (bf16[704,2048]{1,0:T(8,128)(2,1)}, bf16[704,2048]{1,0:T(8,128)(2,1)}, u32[]{:S(2)}, u32[]{:S(2)}) collective-permute-start(bf16[704,2048]{1,0:T(8,128)(2,1)} %collective-permute-done.3), channel_id=1, source_target_pairs={{0,7},{1,0},{2,1},{3,2},{4,3},{5,4},{6,5},{7,6},{8,15},{9,8},{10,9... | collective-permute-start | bytes 8650760 | tf_op jit(solution)/shard_map/ppermute | solution.py:24
  915.3 207.0 %collective-permute-start.6 = (bf16[704,2048]{1,0:T(8,128)(2,1)}, bf16[704,2048]{1,0:T(8,128)(2,1)}, u32[]{:S(2)}, u32[]{:S(2)}) collective-permute-start(bf16[704,2048]{1,0:T(8,128)(2,1)} %collective-permute-done.4), channel_id=1, source_target_pairs={{0,1},{1,2},{2,3},{3,4},{4,5},{5,6},{6,7},{7,0},{8,9},{9,10},{10,1... | collective-permute-start | bytes 8650760 | tf_op jit(solution)/shard_map/ppermute | solution.py:21
  990.2 135.9 %all-to-all-start.1 = ((bf16[4,2,65536]{2,1,0:T(2,128)(2,1)}), bf16[4,2,65536]{2,1,0:T(2,128)(2,1)S(1)}, u32[]{:S(2)}, u32[]{:S(2)}) async-start(bf16[4,2,65536]{2,1,0:T(2,128)(2,1)} %reshape.486), calls=%async_computation.1 | async-start | bytes 2097152 | tf_op jit(solution)/shard_map/all_to_all | solution.py:233
  993.7 2620.0 %reduce-scatter.7.cloned.1.call-start = ((), (), s32[]{:S(2)}) async-start(), calls=%async_computation.11 | async-start | bytes 77856768
  1130.8 781.1 %copy-start.14 = (f32[8,1,256]{2,1,0:T(1,128)S(1)}, f32[8,1,256]{2,1,0:T(1,128)}, u32[]{:S(2)}) copy-start(f32[8,1,256]{2,1,0:T(1,128)} %convert_element_type.151) | copy-start | bytes 24580
  1130.8 781.1 %copy-start.15 = (f32[8,1,256]{2,1,0:T(1,128)S(1)}, f32[8,1,256]{2,1,0:T(1,128)}, u32[]{:S(2)}) copy-start(f32[8,1,256]{2,1,0:T(1,128)} %convert_element_type.152) | copy-start | bytes 24580
  2561.2 18.1 all-to-all-start.2
  2761.1 53.3 %all-to-all-start.3 = ((bf16[1024,3,1,512]{3,1,2,0:T(4,128)(2,1)}), bf16[1024,3,1,512]{3,1,2,0:T(4,128)(2,1)}, u32[]{:S(2)}, u32[]{:S(2)}) async-start(bf16[1024,3,1,512]{3,1,2,0:T(4,128)(2,1)} %copy.126), calls=%async_computation.3 | async-start | bytes 8388608 | tf_op jit(solution)/shard_map/all_to_all | solution.py:300
  2766.2 1389.9 %reduce-scatter.5.cloned.1.call-start = ((), (), s32[]{:S(2)}) async-start(), calls=%async_computation.10 | async-start | bytes 37748736 | tf_op jit(solution)/shard_map/reduce_scatter | solution.py:158
  2861.7 1535.8 %all-reduce.4.cloned.1.call-start = ((), (), s32[]{:S(2)}) async-start(), calls=%async_computation.12 | async-start | bytes 27262976 | tf_op jit(solution)/shard_map/psum | solution.py:316
  (50 other events, 1647.3 us)
Sparse Core Ops, SparseCore 0:
  9.5 798.1 all-gather.9
  809.9 220.9 all-gather.11
  1033.0 878.7 all-gather.13
  1913.2 441.0 all-gather.15
  2528.5 1085.1 reduce-scatter.6
  3617.3 538.7 reduce-scatter.4
  4159.3 238.1 all-reduce.3
